TPU v7x, 32 devices: a whole 2x2x4 slice. The times are simulated.
32 devices in a mesh: groups: 2 (over y), dom: 4 (over z), sub: 2 (over x), field: 2 (over core).
Axes of the slice: x: 2, y: 2, z: 4, core: 2. Of those that a mesh axis runs over, the one named last changes fastest.
Arguments:
- background: float32 [3, 65536], P(None, ('groups', 'dom', 'sub')), parts along dimension 1, may hold values from -6 to 6
- obs_weight: float32 [65536], P(('groups', 'dom', 'sub')), parts along dimension 0, may hold values from 0.02 to 0.2
- connect: int32 [10, 32768], P(None, ('groups', 'dom', 'sub', 'field')), parts along dimension 1, may hold values from 0 to 5631, as said below
- live_blocks: int32 [32], P(('groups', 'dom', 'sub', 'field')), parts along dimension 0, may hold values from 2 to 8, as said below
- elem_scale: float32 [32768], P(('groups', 'dom', 'sub', 'field')), parts along dimension 0, may hold values from 0.5 to 2
- reg_weight: float32 [32768], P(('groups', 'dom', 'sub', 'field')), parts along dimension 0, may hold values from 0.2 to 2
- iterate: float32 [32768], P(('groups', 'dom', 'sub', 'field')), parts along dimension 0, may hold values from -6 to 6
- residual: float32 [32768], P(('groups', 'dom', 'sub', 'field')), parts along dimension 0, may hold values from -30 to 30
- direction: float32 [32768], P(('groups', 'dom', 'sub', 'field')), parts along dimension 0, may hold values from -30 to 30
- send_nodes: int32 [16, 3, 2, 256], P(('groups', 'dom', 'sub')), parts along dimension 0, may hold values from 0 to 4095, as said below
- send_count: int32 [16, 3, 2], P(('groups', 'dom', 'sub')), parts along dimension 0, may hold values from 0 to 256, as said below
- ref_stiff: float32 [30, 30], replicated, may hold values from -1.05 to 4.05, as said below
Outputs:
- iterate_next: float32 [32768], P(('groups', 'dom', 'sub', 'field')), parts along dimension 0
- residual_next: float32 [32768], P(('groups', 'dom', 'sub', 'field')), parts along dimension 0
- direction_next: float32 [32768], P(('groups', 'dom', 'sub', 'field')), parts along dimension 0
There are 2 independent parts, one for each index of `groups`. A program takes and returns all parts, laid end to end along the dimension named above; an argument that names none is the same for every part. Nothing has to cross between parts.
Inputs may be any that keep to these rules, and one draw needn't show every extreme that they name: `send_nodes`: for every link the first send_count slots hold distinct owned nodes; later slots are padding. `send_count`: links go only to partitions of dom index d - 1, d or d + 1 and never to the sender itself or past the ends of dom; some link is full with 256 slots. `connect`: entries from 4096 on name ghost slots that are live slots of their owner's link. `live_blocks`: live blocks fill a device's slots from its first one; some device has 8. `ref_stiff`: Symmetric.
All inputs are finite; a program needn't handle non-finite values.
Results may differ from a plain program's by a relative error of at most 0.00005.
Values sent between devices are 32-bit elements; how exact they have to be, the bound alone decides.
A program may use at most 64 MiB of HBM per device.

v0:
```python
import jax
import jax.numpy as jnp
from jax import lax
from jax.sharding import PartitionSpec as P

BLK = 128


def extended(cells, sides, width):
    for axis, dim in sides:
        count = lax.axis_size(axis)
        ends = count - 1
        head = lax.slice_in_dim(cells, 0, width, axis=dim)
        tail = lax.slice_in_dim(cells, cells.shape[dim] - width, cells.shape[dim], axis=dim)
        cells = jnp.concatenate(
            [
                lax.ppermute(tail, axis, [(i, (i + 1) % count) for i in range(ends)]),
                cells,
                lax.ppermute(head, axis, [((i + 1) % count, i) for i in range(ends)]),
            ],
            axis=dim,
        )
    return cells


def on_device(
    background,
    obs_weight,
    connect,
    live_blocks,
    elem_scale,
    reg_weight,
    iterate,
    residual,
    direction,
    send_nodes,
    send_count,
    ref_stiff,
):
    owned_nodes = background.shape[1]
    sub_count = lax.axis_size("sub")
    link_slots = send_nodes.shape[3]
    element_count = connect.shape[1]
    ghost_slots = 3 * sub_count * link_slots
    targets = send_nodes[0].reshape(-1)
    open_slot = (
        jnp.arange(link_slots, dtype=jnp.int32)[None, None, :] < send_count[0][:, :, None]
    ).astype(jnp.float32)

    def fetch_ghosts(values):
        outbound = values[:, targets].reshape(3, 3, sub_count, link_slots) * open_slot[None]
        mixed = lax.all_to_all(outbound, "sub", split_axis=2, concat_axis=2, tiled=True)
        rimmed = extended(mixed, (("dom", 1),), 1)
        arrived = rimmed[:, 0::2]
        return jnp.concatenate([values, arrived.reshape(3, ghost_slots)], axis=1)

    element = jnp.arange(element_count, dtype=jnp.int32)
    live_mask = (element < BLK * live_blocks[0]).astype(jnp.float32)
    search = live_mask * direction
    remain = live_mask * residual
    guess = live_mask * iterate
    flat_connect = connect.reshape(-1)
    state_full = fetch_ghosts(background)
    element_state = state_full[:, connect].reshape(30, element_count)
    coupled = (live_mask * elem_scale)[None, :] * jnp.dot(
        ref_stiff, element_state, precision=lax.Precision.HIGHEST
    )
    terms = (search[None, :] * coupled).reshape(3, -1)
    accumulated = (
        jnp.zeros((3, owned_nodes + ghost_slots), jnp.float32).at[:, flat_connect].add(terms)
    )
    accumulated = lax.psum(accumulated, "field")
    returning = accumulated[:, owned_nodes:].reshape(3, 3, sub_count, link_slots)
    rimmed = extended(returning, (("dom", 1),), 1)
    landed = lax.all_to_all(rimmed[:, 0::2], "sub", split_axis=2, concat_axis=2, tiled=True)
    landed = (landed * open_slot[None]).reshape(3, -1)
    assembled = accumulated[:, :owned_nodes] + jnp.zeros((3, owned_nodes), jnp.float32).at[
        :, targets
    ].add(landed)
    weighted = obs_weight[None, :] * assembled
    weighted_full = fetch_ghosts(weighted)
    pulled = weighted_full[:, connect].reshape(30, element_count)
    hess_search = jnp.sum(coupled * pulled, axis=0) + reg_weight * search
    squared_before, curvature_sum, cross_term, image_square = lax.psum(
        (
            jnp.sum(remain * remain),
            jnp.sum(search * hess_search),
            jnp.sum(remain * hess_search),
            jnp.sum(hess_search * hess_search),
        ),
        ("dom", "sub", "field"),
    )
    step_length = squared_before / curvature_sum
    iterate_next = guess + step_length * search
    residual_next = remain - step_length * hess_search
    squared_after = (
        squared_before - 2.0 * step_length * cross_term + step_length * step_length * image_square
    )
    direction_next = residual_next + squared_after / squared_before * search
    return (iterate_next, residual_next, direction_next)


def solution(mesh):
    placed = (
        P(None, ("groups", "dom", "sub")),
        P(("groups", "dom", "sub")),
        P(None, ("groups", "dom", "sub", "field")),
        P(("groups", "dom", "sub", "field")),
        P(("groups", "dom", "sub", "field")),
        P(("groups", "dom", "sub", "field")),
        P(("groups", "dom", "sub", "field")),
        P(("groups", "dom", "sub", "field")),
        P(("groups", "dom", "sub", "field")),
        P(("groups", "dom", "sub"), None, None, None),
        P(("groups", "dom", "sub"), None, None),
        P(),
    )
    return jax.shard_map(
        on_device,
        mesh=mesh,
        in_specs=placed,
        out_specs=(
            P(("groups", "dom", "sub", "field")),
            P(("groups", "dom", "sub", "field")),
            P(("groups", "dom", "sub", "field")),
        ),
        check_vma=False,
    )
```

profile of v0, /device:TPU:0, one launch (start us, length us, event | category | flops | bytes accessed | tf_op | source)
XLA Modules:
  0.0 283.6 jit_solution(14023031561616133790)
XLA Ops:
  10.3 2.6 gather_fusion
  13.8 4.2 %all-to-all-start = ((f32[3,3,2,256]{3,1,0,2:T(4,128)}), f32[3,3,2,256]{3,1,0,2:T(4,128)S(1)}, u32[]{:S(2)}, u32[]{:S(2)}) async-start(f32[3,3,2,256]{3,1,0,2:T(4,128)} %broadcast_multiply_fusion.4), calls=%async_computation | async-start | bytes 49152 | tf_op jit(solution)/shard_map/all_to_all | solution.py:52
  18.9 3.1 %all-to-all-done = f32[3,3,2,256]{3,1,0,2:T(4,128)S(1)} async-done(((f32[3,3,2,256]{3,1,0,2:T(4,128)}), f32[3,3,2,256]{3,1,0,2:T(4,128)S(1)}, u32[]{:S(2)}, u32[]{:S(2)}) %all-to-all-start) | async-done | bytes 18464 | tf_op jit(solution)/shard_map/all_to_all | solution.py:52
  22.0 4.0 %collective-permute-start = (f32[3,1,2,256]{3,1,0,2:T(1,128)S(1)}, f32[3,1,2,256]{3,1,0,2:T(1,128)S(1)}, u32[]{:S(2)}, u32[]{:S(2)}) collective-permute-start(f32[3,1,2,256]{3,1,0,2:T(1,128)S(1)} %get-tuple-element.18), channel_id=1, source_target_pairs={{0,4},{4,8},{8,12},{1,5},{5,9},{9,13},{2,6},{6,10},{10,14},{3,7},{... | collective-permute-start | bytes 18440 | tf_op jit(solution)/shard_map/ppermute | solution.py:17
  27.3 4.1 %collective-permute-done.1 = f32[3,1,2,256]{3,1,0,2:T(1,128)S(1)} collective-permute-done((f32[3,1,2,256]{3,1,0,2:T(1,128)S(1)}, f32[3,1,2,256]{3,1,0,2:T(1,128)S(1)}, u32[]{:S(2)}, u32[]{:S(2)}) %collective-permute-start.1) | collective-permute-done | bytes 6176 | tf_op jit(solution)/shard_map/ppermute | solution.py:19
  32.4 34.2 %gather_fusion.1 = f32[10240,3]{1,0:T(8,128)} fusion(f32[3,5632]{0,1:T(8,128)S(1)} %copy.71, s32[10240]{0:T(1024)S(1)} %broadcast_clamp_fusion), kind=kCustom, calls=%fused_computation.1 | custom fusion | bytes 286720 | tf_op jit(solution)/shard_map/gather | solution.py:64
  66.7 4.2 %copy.72 = f32[10,1024,3]{1,0,2:T(8,128)S(1)} copy(f32[10,1024,3]{2,1,0:T(8,128)} %bitcast.28) | data formatting | bytes 245760 | tf_op jit(solution)/shard_map/gather | solution.py:64
  71.3 3.1 %copy.73 = f32[3,10240]{0,1:T(8,128)} copy(f32[3,10240]{1,0:T(4,128)S(1)} %reshape.145) | data formatting | bytes 245760 | tf_op jit(solution)/shard_map/reshape | solution.py:68
  74.4 51.9 %scatter_custom_fusion = f32[3,5632]{0,1:T(8,128)} fusion(s32[10240]{0:T(1024)S(1)} %bitcast.38, f32[3,10240]{0,1:T(8,128)} %copy.73, f32[]{:T(128)} %constant.7.clone.1), kind=kCustom, calls=%fused_computation.6 | custom fusion | flops 30720 | bytes 190468 | tf_op jit(solution)/shard_map/scatter-add | solution.py:70
  126.3 22.2 %all-reduce.3.cloned.1.call-done = f32[3,5632]{0,1:T(8,128)} async-done(((f32[3,5632]{0,1:T(8,128)}), f32[3,5632]{0,1:T(8,128)}) %all-reduce.3.cloned.1.call-update) | async-done | bytes 67600 | tf_op jit(solution)/shard_map/psum | solution.py:72
  150.1 3.8 %collective-permute-start.2 = (f32[3,1,2,256]{3,1,0,2:T(1,128)S(1)}, f32[3,1,2,256]{3,1,0,2:T(1,128)S(1)}, u32[]{:S(2)}, u32[]{:S(2)}) collective-permute-start(f32[3,1,2,256]{3,1,0,2:T(1,128)S(1)} %get-tuple-element.16), channel_id=1, source_target_pairs={{0,4},{4,8},{8,12},{1,5},{5,9},{9,13},{2,6},{6,10},{10,14},{3,7},{... | collective-permute-start | bytes 18440 | tf_op jit(solution)/shard_map/ppermute | solution.py:17
  155.2 4.2 %collective-permute-done.3 = f32[3,1,2,256]{3,1,0,2:T(1,128)S(1)} collective-permute-done((f32[3,1,2,256]{3,1,0,2:T(1,128)S(1)}, f32[3,1,2,256]{3,1,0,2:T(1,128)S(1)}, u32[]{:S(2)}, u32[]{:S(2)}) %collective-permute-start.3) | collective-permute-done | bytes 6176 | tf_op jit(solution)/shard_map/ppermute | solution.py:19
  160.1 3.2 %all-to-all-start.1 = ((f32[3,3,2,256]{3,1,0,2:T(4,128)}), f32[3,3,2,256]{3,1,0,2:T(4,128)S(1)}, u32[]{:S(2)}, u32[]{:S(2)}) async-start(f32[3,3,2,256]{3,1,0,2:T(4,128)} %slice.40), calls=%async_computation.1 | async-start | bytes 49152 | tf_op jit(solution)/shard_map/all_to_all | solution.py:75
  163.4 3.9 %all-to-all-done.1 = f32[3,3,2,256]{3,1,0,2:T(4,128)S(1)} async-done(((f32[3,3,2,256]{3,1,0,2:T(4,128)}), f32[3,3,2,256]{3,1,0,2:T(4,128)S(1)}, u32[]{:S(2)}, u32[]{:S(2)}) %all-to-all-start.1) | async-done | bytes 18464 | tf_op jit(solution)/shard_map/all_to_all | solution.py:75
  167.6 9.5 %scatter_fusion = f32[3,4096]{0,1:T(8,128)S(1)} fusion(f32[3,4096]{0,1:T(8,128)S(1)} %slice-done, s32[1536]{0:T(1024)S(1)} %fusion.5, f32[1536,3]{1,0:T(8,128)S(1)} %copy.78), kind=kCustom, calls=%fused_computation.5 | custom fusion | flops 4608 | bytes 61440 | tf_op jit(solution)/shard_map/scatter-add | solution.py:79
  177.2 1.9 broadcast_multiply_fusion
  179.1 4.3 %gather_fusion.2 = f32[1536,3]{1,0:T(8,128)S(1)} fusion(f32[3,4096]{0,1:T(8,128)} %broadcast_multiply_fusion, s32[2048]{0:T(1024)S(1)} %pad_clamp_fusion), kind=kCustom, calls=%fused_computation.2 | custom fusion | bytes 43008 | tf_op jit(solution)/shard_map/gather | solution.py:51
  183.8 6.3 %all_to_all.15 = f32[3,3,2,256]{3,1,0,2:T(4,128)S(1)} all-to-all(f32[3,3,2,256]{3,1,0,2:T(4,128)S(1)} %broadcast_multiply_fusion.2), channel_id=1, replica_groups=mesh['groups'=2,'dom'=4,'sub'=2,'field'=2] {'sub'}, dimensions={2} | all-to-all | bytes 36864 | tf_op jit(solution)/shard_map/all_to_all | solution.py:52
  190.1 3.4 %collective-permute-start.4 = (f32[3,1,2,256]{3,1,0,2:T(1,128)S(1)}, f32[3,1,2,256]{3,1,0,2:T(1,128)S(1)}, u32[]{:S(2)}, u32[]{:S(2)}) collective-permute-start(f32[3,1,2,256]{3,1,0,2:T(1,128)S(1)} %get-tuple-element.14), channel_id=1, source_target_pairs={{0,4},{4,8},{8,12},{1,5},{5,9},{9,13},{2,6},{6,10},{10,14},{3,7},{... | collective-permute-start | bytes 18440 | tf_op jit(solution)/shard_map/ppermute | solution.py:17
  194.8 4.2 %collective-permute-done.5 = f32[3,1,2,256]{3,1,0,2:T(1,128)S(1)} collective-permute-done((f32[3,1,2,256]{3,1,0,2:T(1,128)S(1)}, f32[3,1,2,256]{3,1,0,2:T(1,128)S(1)}, u32[]{:S(2)}, u32[]{:S(2)}) %collective-permute-start.5) | collective-permute-done | bytes 6176 | tf_op jit(solution)/shard_map/ppermute | solution.py:19
  199.3 1.7 pad_maximum_fusion
  201.1 36.1 %gather_fusion.3 = f32[10240,3]{1,0:T(8,128)} fusion(f32[3,5632]{0,1:T(8,128)} %pad_maximum_fusion, s32[10240]{0:T(1024)S(1)} %broadcast_clamp_fusion), kind=kCustom, calls=%fused_computation.3 | custom fusion | bytes 286720 | tf_op jit(solution)/shard_map/gather | solution.py:82
  237.1 4.2 %copy.84 = f32[10,1024,3]{1,0,2:T(8,128)S(1)} copy(f32[10,1024,3]{2,1,0:T(8,128)} %bitcast.27) | data formatting | bytes 245760 | tf_op jit(solution)/shard_map/gather | solution.py:82
  242.1 30.1 %all-reduce = (f32[]{:T(128)}, f32[]{:T(128)}, f32[]{:T(128)}, f32[]{:T(128)}) all-reduce(f32[]{:T(128)} %get-tuple-element.5, f32[]{:T(128)} %get-tuple-element.6, f32[]{:T(128)} %get-tuple-element.4, f32[]{:T(128)} %get-tuple-element.3), channel_id=1, replica_groups=mesh['groups'=2,'dom'=4,'sub'=2,'field'=2] {'dom','sub','field'}, use_global_device_ids=true, to_apply=%region_1.0 | all-reduce | flops 4 | bytes 32 | tf_op jit(solution)/shard_map/psum | solution.py:84
  (77 shorter events, 13.9 us)
Async XLA Ops:
  7.2 63.8 %copy-start = (f32[30,30]{1,0:T(8,128)S(1)}, f32[30,30]{1,0:T(8,128)}, u32[]{:S(2)}) copy-start(f32[30,30]{1,0:T(8,128)} %param.23) | copy-start | bytes 10804
  7.2 24.4 %copy-start.2 = (f32[3,4096]{1,0:T(4,128)S(1)}, f32[3,4096]{1,0:T(4,128)}, u32[]{:S(2)}) copy-start(f32[3,4096]{1,0:T(4,128)} %param.12) | copy-start | bytes 147460
  7.2 10.9 %copy-start.3 = (s32[10,1024]{1,0:T(8,128)S(1)}, s32[10,1024]{1,0:T(8,128)}, u32[]{:S(2)}) copy-start(s32[10,1024]{1,0:T(8,128)} %param.14) | copy-start | bytes 122884
  7.2 20.0 %copy-start.7 = (f32[1024]{0:T(1024)S(1)}, f32[1024]{0:T(1024)}, u32[]{:S(2)}) copy-start(f32[1024]{0:T(1024)} %param.20) | copy-start | bytes 12292
  7.2 20.0 %copy-start.6 = (f32[1024]{0:T(1024)S(1)}, f32[1024]{0:T(1024)}, u32[]{:S(2)}) copy-start(f32[1024]{0:T(1024)} %param.16) | copy-start | bytes 12292
  13.8 8.1 %all-to-all-start = ((f32[3,3,2,256]{3,1,0,2:T(4,128)}), f32[3,3,2,256]{3,1,0,2:T(4,128)S(1)}, u32[]{:S(2)}, u32[]{:S(2)}) async-start(f32[3,3,2,256]{3,1,0,2:T(4,128)} %broadcast_multiply_fusion.4), calls=%async_computation | async-start | bytes 49152 | tf_op jit(solution)/shard_map/all_to_all | solution.py:52
  18.1 130.5 %all-reduce.3.cloned.1.call-start = ((), (), s32[]{:S(2)}) async-start(), calls=%async_computation.3 | async-start | bytes 5767168 | tf_op jit(solution)/shard_map/psum | solution.py:72
  22.0 5.3 %collective-permute-start = (f32[3,1,2,256]{3,1,0,2:T(1,128)S(1)}, f32[3,1,2,256]{3,1,0,2:T(1,128)S(1)}, u32[]{:S(2)}, u32[]{:S(2)}) collective-permute-start(f32[3,1,2,256]{3,1,0,2:T(1,128)S(1)} %get-tuple-element.18), channel_id=1, source_target_pairs={{0,4},{4,8},{8,12},{1,5},{5,9},{9,13},{2,6},{6,10},{10,14},{3,7},{... | collective-permute-start | bytes 18440 | tf_op jit(solution)/shard_map/ppermute | solution.py:17
  25.9 5.5 %collective-permute-start.1 = (f32[3,1,2,256]{3,1,0,2:T(1,128)S(1)}, f32[3,1,2,256]{3,1,0,2:T(1,128)S(1)}, u32[]{:S(2)}, u32[]{:S(2)}) collective-permute-start(f32[3,1,2,256]{3,1,0,2:T(1,128)S(1)} %get-tuple-element.19), channel_id=1, source_target_pairs={{4,0},{8,4},{12,8},{5,1},{9,5},{13,9},{6,2},{10,6},{14,10},{7,3},{... | collective-permute-start | bytes 18440 | tf_op jit(solution)/shard_map/ppermute | solution.py:19
  150.1 17.5 %slice-start = ((f32[3,5632]{0,1:T(8,128)}), f32[3,4096]{0,1:T(8,128)S(1)}, s32[]{:S(2)}) async-start(f32[3,5632]{0,1:T(8,128)} %all-reduce.3.cloned.1.call-done), calls=%async_computation.4 | async-start | bytes 4194304 | tf_op jit(solution)/shard_map/slice | solution.py:77
  150.1 27.0 %copy-start.4 = (f32[4096]{0:T(1024)S(1)}, f32[4096]{0:T(1024)}, u32[]{:S(2)}) copy-start(f32[4096]{0:T(1024)} %param.13) | copy-start | bytes 49156
  150.1 5.1 %collective-permute-start.2 = (f32[3,1,2,256]{3,1,0,2:T(1,128)S(1)}, f32[3,1,2,256]{3,1,0,2:T(1,128)S(1)}, u32[]{:S(2)}, u32[]{:S(2)}) collective-permute-start(f32[3,1,2,256]{3,1,0,2:T(1,128)S(1)} %get-tuple-element.16), channel_id=1, source_target_pairs={{0,4},{4,8},{8,12},{1,5},{5,9},{9,13},{2,6},{6,10},{10,14},{3,7},{... | collective-permute-start | bytes 18440 | tf_op jit(solution)/shard_map/ppermute | solution.py:17
  153.9 5.5 %collective-permute-start.3 = (f32[3,1,2,256]{3,1,0,2:T(1,128)S(1)}, f32[3,1,2,256]{3,1,0,2:T(1,128)S(1)}, u32[]{:S(2)}, u32[]{:S(2)}) collective-permute-start(f32[3,1,2,256]{3,1,0,2:T(1,128)S(1)} %get-tuple-element.17), channel_id=1, source_target_pairs={{4,0},{8,4},{12,8},{5,1},{9,5},{13,9},{6,2},{10,6},{14,10},{7,3},{... | collective-permute-start | bytes 18440 | tf_op jit(solution)/shard_map/ppermute | solution.py:19
  160.1 7.1 %all-to-all-start.1 = ((f32[3,3,2,256]{3,1,0,2:T(4,128)}), f32[3,3,2,256]{3,1,0,2:T(4,128)S(1)}, u32[]{:S(2)}, u32[]{:S(2)}) async-start(f32[3,3,2,256]{3,1,0,2:T(4,128)} %slice.40), calls=%async_computation.1 | async-start | bytes 49152 | tf_op jit(solution)/shard_map/all_to_all | solution.py:75
  179.1 20.2 %copy-start.1 = (f32[3,4096]{0,1:T(8,128)S(1)}, f32[3,4096]{0,1:T(8,128)}, u32[]{:S(2)}) copy-start(f32[3,4096]{0,1:T(8,128)} %broadcast_multiply_fusion) | copy-start | bytes 147460
  190.1 4.7 %collective-permute-start.4 = (f32[3,1,2,256]{3,1,0,2:T(1,128)S(1)}, f32[3,1,2,256]{3,1,0,2:T(1,128)S(1)}, u32[]{:S(2)}, u32[]{:S(2)}) collective-permute-start(f32[3,1,2,256]{3,1,0,2:T(1,128)S(1)} %get-tuple-element.14), channel_id=1, source_target_pairs={{0,4},{4,8},{8,12},{1,5},{5,9},{9,13},{2,6},{6,10},{10,14},{3,7},{... | collective-permute-start | bytes 18440 | tf_op jit(solution)/shard_map/ppermute | solution.py:17
  193.5 5.5 %collective-permute-start.5 = (f32[3,1,2,256]{3,1,0,2:T(1,128)S(1)}, f32[3,1,2,256]{3,1,0,2:T(1,128)S(1)}, u32[]{:S(2)}, u32[]{:S(2)}) collective-permute-start(f32[3,1,2,256]{3,1,0,2:T(1,128)S(1)} %get-tuple-element.15), channel_id=1, source_target_pairs={{4,0},{8,4},{12,8},{5,1},{9,5},{13,9},{6,2},{10,6},{14,10},{7,3},{... | collective-permute-start | bytes 18440 | tf_op jit(solution)/shard_map/ppermute | solution.py:19
  237.1 4.3 %copy-start.5 = (f32[1024]{0:T(1024)S(1)}, f32[1024]{0:T(1024)}, u32[]{:S(2)}) copy-start(f32[1024]{0:T(1024)} %param.19) | copy-start | bytes 12292
  237.1 4.3 %copy-start.8 = (f32[1024]{0:T(1024)S(1)}, f32[1024]{0:T(1024)}, u32[]{:S(2)}) copy-start(f32[1024]{0:T(1024)} %param.17) | copy-start | bytes 12292
  237.1 39.0 %copy-start.9 = (f32[1024]{0:T(1024)S(1)}, f32[1024]{0:T(1024)}, u32[]{:S(2)}) copy-start(f32[1024]{0:T(1024)} %param.18) | copy-start | bytes 12292
Sparse Core Ops, SparseCore 0:
  126.4 22.0 all-reduce.2
where the time goes:
time: 284 us
  local copies, waits for them, and re-layouts  95.7 us (34%)
  other arithmetic  67.9 us (24%)
  waiting for transfers between devices  41.8 us (15%)
  blocking collectives  36.4 us (13%)
  starting transfers between devices  22.5 us (8%)
  between operations  19.1 us (7%)
    scatter-add x1, other arithmetic, on_device(): jnp.zeros((3, owned_nodes + ghost_slots), jnp.float32).at[:, flat_connect]  51.9 us
    gather x2, local copies, waits for them, and re-layouts, on_device(): pulled = weighted_full[:, connect].reshape(30, element_count)  40.3 us
    gather x2, local copies, waits for them, and re-layouts, on_device(): element_state = state_full[:, connect].reshape(30, element_count)  38.4 us
    psum x1, blocking collectives, on_device(): lax.psum((jnp.sum(remain * remain), jnp.sum(search * hess_search), jnp.su...  30.1 us
    psum x1, waiting for transfers between devices, on_device(): accumulated = lax.psum(accumulated, 'field')  22.2 us
    ppermute x3, waiting for transfers between devices, extended(): lax.ppermute(head, axis, [((i + 1) % count, i) for i in range(ends)])  12.5 us
    ppermute x3, starting transfers between devices, extended(): lax.ppermute(tail, axis, [(i, (i + 1) % count) for i in range(ends)])  11.2 us
    scatter-add x1, other arithmetic, on_device(): assembled = accumulated[:, :owned_nodes] + jnp.zeros((3, owned_nodes), jn...  9.52 us
  transfers between devices with their start and end apart: 9, of which 6 were waited for; matrix products, arithmetic and copies ran while one was open for 0% of the time, Pallas kernels for 0%

commit v1 on v0

v1 whole, which is shorter than its diff:
```python
import functools

import jax
import jax.numpy as jnp
from jax import lax
from jax.experimental import pallas as pl
from jax.experimental.pallas import tpu as pltpu
from jax.sharding import PartitionSpec as P

BLK = 128
LANES = 128
F32 = jnp.float32
BF16 = jnp.bfloat16
MESH = pl.DeviceIdType.MESH


def split(values):
    high = values.astype(BF16)
    return high, (values - high.astype(F32)).astype(BF16)


def low_hot(index):
    rows = lax.broadcasted_iota(jnp.int32, (LANES, index.shape[1]), 0)
    return jnp.where(rows == (index & (LANES - 1)), 1.0, 0.0).astype(BF16)


def high_mask(index, rows):
    return lax.broadcasted_iota(jnp.int32, (rows, index.shape[1]), 0) == (index >> 7)


def picked(table, rows, index):
    hot = low_hot(index)
    wide = jnp.dot(table, jnp.concatenate([hot, hot], axis=0), preferred_element_type=F32)
    mask = high_mask(index, rows)
    return [jnp.where(mask, wide[c * rows : (c + 1) * rows], 0.0) for c in range(3)]


def spread(values, index, rows):
    mask = high_mask(index, rows)
    pieces = [split(v) for v in values]
    blocks = []
    for p in range(2):
        for c in range(3):
            piece = jnp.broadcast_to(pieces[c][p].astype(F32), mask.shape)
            blocks.append(jnp.where(mask, piece, 0.0).astype(BF16))
    return lax.dot_general(
        jnp.concatenate(blocks, axis=0),
        low_hot(index),
        (((1,), (1,)), ((), ())),
        preferred_element_type=F32,
    )


def kernel(
    doms,
    subs,
    fields,
    stages,
    background,
    obs_weight,
    connect,
    live_blocks,
    elem_scale,
    reg_weight,
    iterate,
    residual,
    direction,
    send_nodes,
    send_count,
    ref_stiff,
    iterate_next,
    residual_next,
    direction_next,
    table_f,
    table,
    state,
    coupled,
    acc,
    own,
    own_in,
    out_a,
    in_a,
    out_b,
    in_b,
    ret,
    ret_in,
    red,
    red_in,
    sems_a,
    sems_b,
    sems_r,
    sems_x,
    sems_s,
):
    d, s, f = (lax.axis_index(a) for a in ("dom", "sub", "field"))
    elements = connect.shape[1]
    link = send_nodes.shape[3]
    own_rows = obs_weight.shape[0]
    rows = table_f.shape[1]
    per_link = link // LANES
    links = [(o, t) for o in range(3) for t in range(subs) if (o, t) != (1, 0)]

    def at(dd, ds, df):
        return {
            "dom": lax.rem(d + dd + doms, doms),
            "sub": lax.rem(s + ds, subs),
            "field": lax.rem(f + df, fields),
        }

    def when(o, step):
        if o == 0:
            pl.when(d > 0)(step)
        elif o == 2:
            pl.when(d < doms - 1)(step)
        else:
            step()

    greeted = {(dd % doms, ds, df) for dd in (-1, 0, 1) for ds in range(subs) for df in range(fields)}
    for stage in stages:
        greeted |= set(stage)
    greeted = sorted(greeted - {(0, 0, 0)})

    in_a[...] = jnp.zeros_like(in_a)
    in_b[...] = jnp.zeros_like(in_b)
    ret_in[...] = jnp.zeros_like(ret_in)
    barrier = pltpu.get_barrier_semaphore()
    for offset in greeted:
        pl.semaphore_signal(barrier, inc=1, device_id=at(*offset), device_id_type=MESH)

    table_f[...] = jnp.zeros_like(table_f)
    for r in range(own_rows):
        table_f[:, r, :] = background[:, r * LANES : (r + 1) * LANES]

    def fill_table(part):
        for c in range(3):
            high, low = split(table_f[c])
            table[c * rows : (c + 1) * rows, :LANES] = high
            table[c * rows : (c + 1) * rows, LANES:] = low

    def outbound(out):
        for o in range(3):
            for t in range(subs):
                index = send_nodes[0, o, t : t + 1, :]
                slot = lax.broadcasted_iota(jnp.int32, index.shape, 1)
                open_slot = jnp.where(slot < send_count[0, o, t], 1.0, 0.0)
                for c, wide in enumerate(picked(table[...], rows, index)):
                    out[o * subs + t, c : c + 1, :] = open_slot * jnp.sum(wide, axis=0, keepdims=True)

    def ghost_copy(o, t, out, landing, sems):
        return pltpu.make_async_remote_copy(
            src_ref=out.at[o * subs + lax.rem(s + t, subs)],
            dst_ref=landing.at[(2 - o) * subs + s],
            send_sem=sems.at[0, o * subs + t],
            recv_sem=sems.at[1, (2 - o) * subs + (subs - t) % subs],
            device_id=at(o - 1, t, 0),
            device_id_type=MESH,
        )

    def ghost_arrival(o, t, out, landing, sems):
        return pltpu.make_async_remote_copy(
            src_ref=out.at[o * subs + lax.rem(s + t, subs)],
            dst_ref=landing.at[o * subs + lax.rem(s + t, subs)],
            send_sem=sems.at[0, o * subs + t],
            recv_sem=sems.at[1, o * subs + t],
            device_id=at(o - 1, t, 0),
            device_id_type=MESH,
        )

    def exchange(out, landing, sems):
        for o, t in links:
            when(o, lambda o=o, t=t: ghost_copy(o, t, out, landing, sems).start())
        for o, t in links:
            when(o, lambda o=o, t=t: ghost_arrival(o, t, out, landing, sems).wait_recv())
        for o, t in links:
            when(o, lambda o=o, t=t: ghost_copy(o, t, out, landing, sems).wait_send())

    def ghosts_in(landing):
        for q in range(3 * subs):
            for h in range(per_link):
                table_f[:, own_rows + q * per_link + h, :] = landing[q, :, h * LANES : (h + 1) * LANES]

    fill_table(0)
    outbound(out_a)
    pl.semaphore_wait(barrier, len(greeted))
    exchange(out_a, in_a, sems_a)
    ghosts_in(in_a)
    fill_table(1)

    element = lax.broadcasted_iota(jnp.int32, (1, elements), 1)
    live = jnp.where(element < BLK * live_blocks[0], 1.0, 0.0)
    search = live * direction[...]
    remain = live * residual[...]
    guess = live * iterate[...]
    nodes = connect.shape[0]

    def pull(k, carry):
        index = connect[pl.ds(k, 1), :]
        for c, wide in enumerate(picked(table[...], rows, index)):
            state[pl.ds(c * nodes + k, 1), :] = jnp.sum(wide, axis=0, keepdims=True)
        return carry

    lax.fori_loop(0, nodes, pull, 0)
    coupled[...] = (live * elem_scale[...]) * jnp.dot(
        ref_stiff[...], state[...], precision=lax.Precision.HIGHEST, preferred_element_type=F32
    )

    acc[...] = jnp.zeros_like(acc)

    def push(k, carry):
        index = connect[pl.ds(k, 1), :]
        terms = [search * coupled[pl.ds(c * nodes + k, 1), :] for c in range(3)]
        acc[...] += spread(terms, index, rows)
        return carry

    lax.fori_loop(0, nodes, push, 0)
    for c in range(3):
        total = acc[c * rows : (c + 1) * rows, :] + acc[(3 + c) * rows : (4 + c) * rows, :]
        own[c] = total[:own_rows]
        for q in range(3 * subs):
            for h in range(per_link):
                r = own_rows + q * per_link + h
                ret[q, c : c + 1, h * LANES : (h + 1) * LANES] = total[r : r + 1]

    def ret_copy(o, t, g):
        return pltpu.make_async_remote_copy(
            src_ref=ret.at[o * subs + lax.rem(s + t, subs)],
            dst_ref=ret_in.at[g, (2 - o) * subs + s],
            send_sem=sems_r.at[0, g, o * subs + t],
            recv_sem=sems_r.at[1, g, (2 - o) * subs + (subs - t) % subs],
            device_id=at(o - 1, t, g),
            device_id_type=MESH,
        )

    def ret_arrival(o, t, g):
        return pltpu.make_async_remote_copy(
            src_ref=ret.at[o * subs + lax.rem(s + t, subs)],
            dst_ref=ret_in.at[g, o * subs + lax.rem(s + t, subs)],
            send_sem=sems_r.at[0, g, o * subs + t],
            recv_sem=sems_r.at[1, g, o * subs + t],
            device_id=at(o - 1, t, g),
            device_id_type=MESH,
        )

    def own_copy(g):
        return pltpu.make_async_remote_copy(
            src_ref=own,
            dst_ref=own_in.at[g - 1],
            send_sem=sems_x.at[0, g - 1],
            recv_sem=sems_x.at[1, g - 1],
            device_id=at(0, 0, g),
            device_id_type=MESH,
        )

    for o, t in links:
        for g in range(fields):
            when(o, lambda o=o, t=t, g=g: ret_copy(o, t, g).start())
    for g in range(1, fields):
        own_copy(g).start()
    for o, t in links:
        for g in range(fields):
            when(o, lambda o=o, t=t, g=g: ret_arrival(o, t, g).wait_recv())
    landed = None
    for o in range(3):
        for t in range(subs):
            q = o * subs + t
            index = send_nodes[0, o, t : t + 1, :]
            slot = lax.broadcasted_iota(jnp.int32, index.shape, 1)
            open_slot = jnp.where(slot < send_count[0, o, t], 1.0, 0.0)
            sums = ret_in[0, q]
            for g in range(1, fields):
                sums = sums + ret_in[g, q]
            part = spread([open_slot * sums[c : c + 1] for c in range(3)], index, own_rows)
            landed = part if landed is None else landed + part
    for g in range(1, fields):
        own_copy(g).wait_recv()
    for c in range(3):
        assembled = own[c]
        for g in range(1, fields):
            assembled = assembled + own_in[g - 1, c]
        assembled = assembled + landed[c * own_rows : (c + 1) * own_rows]
        assembled = assembled + landed[(3 + c) * own_rows : (4 + c) * own_rows]
        table_f[c, :own_rows, :] = obs_weight[...] * assembled

    fill_table(0)
    outbound(out_b)
    exchange(out_b, in_b, sems_b)
    ghosts_in(in_b)
    fill_table(1)

    def back(k, total):
        index = connect[pl.ds(k, 1), :]
        for c, wide in enumerate(picked(table[...], rows, index)):
            total = total + coupled[pl.ds(c * nodes + k, 1), :] * jnp.sum(wide, axis=0, keepdims=True)
        return total

    hess = lax.fori_loop(0, nodes, back, jnp.zeros((1, elements), F32)) + reg_weight[...] * search

    def lane_sums(values):
        total = values[:, :LANES]
        for e in range(LANES, elements, LANES):
            total = total + values[:, e : e + LANES]
        return total

    red[0] = jnp.concatenate(
        [lane_sums(v) for v in (remain * remain, search * hess, remain * hess, hess * hess)]
        + [jnp.zeros((4, LANES), F32)],
        axis=0,
    )
    first = 0
    for n, stage in enumerate(stages):

        def red_copy(i, offset, n=n, first=first):
            return pltpu.make_async_remote_copy(
                src_ref=red.at[n],
                dst_ref=red_in.at[first + i],
                send_sem=sems_s.at[0, first + i],
                recv_sem=sems_s.at[1, first + i],
                device_id=at(*offset),
                device_id_type=MESH,
            )

        for i, offset in enumerate(stage):
            red_copy(i, offset).start()
        total = red[n]
        for i, offset in enumerate(stage):
            red_copy(i, offset).wait_recv()
            total = total + red_in[first + i]
        for i, offset in enumerate(stage):
            red_copy(i, offset).wait_send()
        red[n + 1] = total
        first += len(stage)
    sums = jnp.sum(red[len(stages)], axis=1, keepdims=True)
    before, curvature, cross, image = (sums[i : i + 1] for i in range(4))
    step = before / curvature
    after = before - 2.0 * step * cross + step * step * image
    remain_next = remain - step * hess
    iterate_next[...] = guess + step * search
    residual_next[...] = remain_next
    direction_next[...] = remain_next + (after / before) * search
    for o, t in links:
        for g in range(fields):
            when(o, lambda o=o, t=t, g=g: ret_copy(o, t, g).wait_send())
    for g in range(1, fields):
        own_copy(g).wait_send()


def solution(mesh):
    doms, subs, fields = (mesh.shape[a] for a in ("dom", "sub", "field"))
    whole = [(a, b, c) for a in range(doms) for b in range(subs) for c in range(fields)]
    whole = whole[1:]
    if len(whole) < 32:
        stages = [whole]
    else:
        stages = [[w for w in whole if w[0] == 0], [w for w in whole if w[1:] == (0, 0)]]

    def on_device(
        background,
        obs_weight,
        connect,
        live_blocks,
        elem_scale,
        reg_weight,
        iterate,
        residual,
        direction,
        send_nodes,
        send_count,
        ref_stiff,
    ):
        elements = connect.shape[1]
        link = send_nodes.shape[3]
        own_rows = background.shape[1] // LANES
        links = 3 * subs
        rows = -(-(own_rows + links * link // LANES) // 16) * 16
        vmem = pl.BlockSpec(memory_space=pltpu.VMEM)
        smem = pl.BlockSpec(memory_space=pltpu.SMEM)
        partners = sum(len(stage) for stage in stages)
        outs = pl.pallas_call(
            functools.partial(kernel, doms, subs, fields, stages),
            out_shape=[jax.ShapeDtypeStruct((1, elements), F32)] * 3,
            in_specs=[vmem, vmem, vmem, smem, vmem, vmem, vmem, vmem, vmem, vmem, smem, vmem],
            out_specs=[vmem] * 3,
            scratch_shapes=[
                pltpu.VMEM((3, rows, LANES), F32),
                pltpu.VMEM((3 * rows, 2 * LANES), BF16),
                pltpu.VMEM((3 * connect.shape[0], elements), F32),
                pltpu.VMEM((3 * connect.shape[0], elements), F32),
                pltpu.VMEM((6 * rows, LANES), F32),
                pltpu.VMEM((3, own_rows, LANES), F32),
                pltpu.VMEM((max(fields - 1, 1), 3, own_rows, LANES), F32),
                pltpu.VMEM((links, 3, link), F32),
                pltpu.VMEM((links, 3, link), F32),
                pltpu.VMEM((links, 3, link), F32),
                pltpu.VMEM((links, 3, link), F32),
                pltpu.VMEM((links, 3, link), F32),
                pltpu.VMEM((fields, links, 3, link), F32),
                pltpu.VMEM((len(stages) + 1, 8, LANES), F32),
                pltpu.VMEM((partners, 8, LANES), F32),
                pltpu.SemaphoreType.DMA((2, links)),
                pltpu.SemaphoreType.DMA((2, links)),
                pltpu.SemaphoreType.DMA((2, fields, links)),
                pltpu.SemaphoreType.DMA((2, max(fields - 1, 1))),
                pltpu.SemaphoreType.DMA((2, partners)),
            ],
            compiler_params=pltpu.CompilerParams(
                collective_id=0, has_side_effects=True, vmem_limit_bytes=48 * 1024 * 1024
            ),
        )(
            background,
            obs_weight.reshape(own_rows, LANES),
            connect,
            live_blocks,
            elem_scale.reshape(1, elements),
            reg_weight.reshape(1, elements),
            iterate.reshape(1, elements),
            residual.reshape(1, elements),
            direction.reshape(1, elements),
            send_nodes,
            send_count,
            ref_stiff,
        )
        return tuple(x.reshape(elements) for x in outs)

    owned = P(("groups", "dom", "sub"))
    element = P(("groups", "dom", "sub", "field"))
    return jax.shard_map(
        on_device,
        mesh=mesh,
        in_specs=(
            P(None, ("groups", "dom", "sub")),
            owned,
            P(None, ("groups", "dom", "sub", "field")),
            element,
            element,
            element,
            element,
            element,
            element,
            P(("groups", "dom", "sub"), None, None, None),
            P(("groups", "dom", "sub"), None, None),
            P(),
        ),
        out_specs=(element, element, element),
        check_vma=False,
    )
```

time: 284 us -> 42.2 us (0.15)
  local copies, waits for them, and re-layouts: 95.7 us -> 9.07 us
  other arithmetic: 67.9 us -> 0 us
  waiting for transfers between devices: 41.8 us -> 0 us
  blocking collectives: 36.4 us -> 0 us
  Pallas kernels: 0 us -> 31.3 us
  starting transfers between devices: 22.5 us -> 0 us
  between operations: 19.1 us -> 1.32 us
    gather x6 -> x0, local copies, waits for them, and re-layouts: 85.7 us -> none  [the longest x2 40.3 us: on_device(): pulled = weighted_full[:, connect].reshape(30, element_count)]
    scatter-add x2 -> x0, other arithmetic: 61.4 us -> none  [the longest x1 51.9 us: on_device(): jnp.zeros((3, owned_nodes + ghost_slots), jnp.float32).at[:, flat_connect]]
    pallas_call x0 -> x1, Pallas kernels: none -> 31.3 us  [on_device(): pl.pallas_call(functools.partial(kernel, doms, subs, fields, stages), out...]
    psum x1 -> x0, blocking collectives: 30.1 us -> none  [on_device(): lax.psum((jnp.sum(remain * remain), jnp.sum(search * hess_search), jnp.su...]
    psum x1 -> x0, waiting for transfers between devices: 22.2 us -> none  [on_device(): accumulated = lax.psum(accumulated, 'field')]
    ppermute x6 -> x0, starting transfers between devices: 15 us -> none  [the longest x3 11.2 us: extended(): lax.ppermute(tail, axis, [(i, (i + 1) % count) for i in range(ends)])]
    ppermute x6 -> x0, waiting for transfers between devices: 12.6 us -> none  [the longest x3 12.5 us: extended(): lax.ppermute(head, axis, [((i + 1) % count, i) for i in range(ends)])]
    unnamed x22 -> x24, local copies, waits for them, and re-layouts: 1.57 us -> 9.07 us
  transfers between devices with their start and end apart: 9 -> 0, of which waited for: 6 -> 0; matrix products, arithmetic and copies ran while one was open for 0% -> 0% of each run, Pallas kernels for 0% -> 0%
where the time goes in v1:
time: 42.2 us; the launch traced here: 41.7 us
  Pallas kernels  31.3 us (74%)
  local copies, waits for them, and re-layouts  9.07 us (21%)
  between operations  1.32 us (3%)
    pallas_call x1, Pallas kernels, on_device(): pl.pallas_call(functools.partial(kernel, doms, subs, fields, stages), out...  31.3 us
    unnamed x24, local copies, waits for them, and re-layouts  9.07 us

profile of v1, /device:TPU:0, one launch (start us, length us, event | category | flops | bytes accessed | tf_op | source)
XLA Modules:
  0.0 41.7 jit_solution(898168209360023008)
XLA Ops:
  0.6 0.0 copy-start.2
  1.3 0.8 %copy.15.send_count = s32[1,3,2]{2,1,0:T(4,128)S(1)} copy(s32[1,3,2]{1,2,0:T(2,128)} %param.22) | data formatting | bytes 48 | tf_op args[10]
  2.1 0.0 copy-done.2
  2.1 0.0 copy-start
  2.1 0.8 %copy-done = f32[3,4096]{1,0:T(4,128)S(1)} copy-done((f32[3,4096]{1,0:T(4,128)S(1)}, f32[3,4096]{1,0:T(4,128)}, u32[]{:S(2)}) %copy-start) | copy-done | bytes 49176
  2.9 0.0 copy-start.1
  2.9 0.8 %copy-done.1 = s32[10,1024]{1,0:T(8,128)S(1)} copy-done((s32[10,1024]{1,0:T(8,128)S(1)}, s32[10,1024]{1,0:T(8,128)}, u32[]{:S(2)}) %copy-start.1) | copy-done | bytes 40984
  3.7 0.0 copy-start.3
  3.8 0.7 %copy-done.3 = f32[30,30]{1,0:T(8,128)S(1)} copy-done((f32[30,30]{1,0:T(8,128)S(1)}, f32[30,30]{1,0:T(8,128)}, u32[]{:S(2)}) %copy-start.3) | copy-done | bytes 3624
  4.5 0.0 copy-start.4
  4.5 0.7 %copy-done.4 = s32[1,3,2,256]{3,2,1,0:T(2,128)S(1)} copy-done((s32[1,3,2,256]{3,2,1,0:T(2,128)S(1)}, s32[1,3,2,256]{3,2,1,0:T(2,128)}, u32[]{:S(2)}) %copy-start.4) | copy-done | bytes 6168
  5.2 0.0 copy-start.5
  5.2 0.7 %copy-done.5 = f32[1024]{0:T(1024)S(1)} copy-done((f32[1024]{0:T(1024)S(1)}, f32[1024]{0:T(1024)}, u32[]{:S(2)}) %copy-start.5) | copy-done | bytes 4120
  5.8 0.0 copy-start.6
  5.8 0.7 %copy-done.6 = f32[1024]{0:T(1024)S(1)} copy-done((f32[1024]{0:T(1024)S(1)}, f32[1024]{0:T(1024)}, u32[]{:S(2)}) %copy-start.6) | copy-done | bytes 4120
  6.5 0.7 %copy-done.7 = f32[1024]{0:T(1024)S(1)} copy-done((f32[1024]{0:T(1024)S(1)}, f32[1024]{0:T(1024)}, u32[]{:S(2)}) %copy-start.7) | copy-done | bytes 4120
  7.2 0.0 copy-start.8
  7.2 0.7 %copy-done.8 = f32[1024]{0:T(1024)S(1)} copy-done((f32[1024]{0:T(1024)S(1)}, f32[1024]{0:T(1024)}, u32[]{:S(2)}) %copy-start.8) | copy-done | bytes 4120
  7.9 0.0 copy-start.9
  7.9 0.7 %copy-done.9 = f32[1024]{0:T(1024)S(1)} copy-done((f32[1024]{0:T(1024)S(1)}, f32[1024]{0:T(1024)}, u32[]{:S(2)}) %copy-start.9) | copy-done | bytes 4120
  8.6 31.3 %shard_map.139 = (f32[1,1024]{1,0:T(1,128)S(1)}, f32[1,1024]{1,0:T(1,128)S(1)}, f32[1,1024]{1,0:T(1,128)S(1)}) custom-call(f32[3,4096]{1,0:T(4,128)S(1)} %copy-done, f32[32,128]{1,0:T(8,128)S(1)} %bitcast.9, s32[10,1024]{1,0:T(8,128)S(1)} %copy-done.1, s32[1]{0:T(128)S(6)} %copy.19.live_blocks, f32[1,1024]{1,0:T(1,128)S(1)} %bitcast.10, ...), custom_call_target="tpu_custom_call" | custom-call | tf_op jit(solution)/shard_map/pallas_call | solution.py:378
  39.9 0.6 %copy.20 = f32[1024]{0:T(1024)} copy(f32[1024]{0:T(1024)S(1)} %bitcast.17) | data formatting | bytes 8192
  40.5 0.6 %copy.21 = f32[1024]{0:T(1024)} copy(f32[1024]{0:T(1024)S(1)} %bitcast.16) | data formatting | bytes 8192
  41.1 0.6 %copy.22 = f32[1024]{0:T(1024)} copy(f32[1024]{0:T(1024)S(1)} %bitcast.15) | data formatting | bytes 8192
  (1 shorter events, 0.0 us)
Async XLA Ops:
  0.6 1.4 %copy-start.2 = (f32[4096]{0:T(1024)S(1)}, f32[4096]{0:T(1024)}, u32[]{:S(2)}) copy-start(f32[4096]{0:T(1024)} %param.13) | copy-start | bytes 49156
  2.1 0.8 %copy-start = (f32[3,4096]{1,0:T(4,128)S(1)}, f32[3,4096]{1,0:T(4,128)}, u32[]{:S(2)}) copy-start(f32[3,4096]{1,0:T(4,128)} %background.1) | copy-start | bytes 147460
  2.9 0.8 %copy-start.1 = (s32[10,1024]{1,0:T(8,128)S(1)}, s32[10,1024]{1,0:T(8,128)}, u32[]{:S(2)}) copy-start(s32[10,1024]{1,0:T(8,128)} %connect.1) | copy-start | bytes 122884
  3.7 0.7 %copy-start.3 = (f32[30,30]{1,0:T(8,128)S(1)}, f32[30,30]{1,0:T(8,128)}, u32[]{:S(2)}) copy-start(f32[30,30]{1,0:T(8,128)} %ref_stiff.1) | copy-start | bytes 10804
  4.5 0.7 %copy-start.4 = (s32[1,3,2,256]{3,2,1,0:T(2,128)S(1)}, s32[1,3,2,256]{3,2,1,0:T(2,128)}, u32[]{:S(2)}) copy-start(s32[1,3,2,256]{3,2,1,0:T(2,128)} %send_nodes.1) | copy-start | bytes 18436
  5.2 0.7 %copy-start.5 = (f32[1024]{0:T(1024)S(1)}, f32[1024]{0:T(1024)}, u32[]{:S(2)}) copy-start(f32[1024]{0:T(1024)} %param.16) | copy-start | bytes 12292
  5.8 0.7 %copy-start.6 = (f32[1024]{0:T(1024)S(1)}, f32[1024]{0:T(1024)}, u32[]{:S(2)}) copy-start(f32[1024]{0:T(1024)} %param.17) | copy-start | bytes 12292
  6.5 0.7 %copy-start.7 = (f32[1024]{0:T(1024)S(1)}, f32[1024]{0:T(1024)}, u32[]{:S(2)}) copy-start(f32[1024]{0:T(1024)} %param.18) | copy-start | bytes 12292
  7.2 0.7 %copy-start.8 = (f32[1024]{0:T(1024)S(1)}, f32[1024]{0:T(1024)}, u32[]{:S(2)}) copy-start(f32[1024]{0:T(1024)} %param.19) | copy-start | bytes 12292
  7.9 0.7 %copy-start.9 = (f32[1024]{0:T(1024)S(1)}, f32[1024]{0:T(1024)}, u32[]{:S(2)}) copy-start(f32[1024]{0:T(1024)} %param.20) | copy-start | bytes 12292

commit v2 on v1

--- a/solution.py
+++ b/solution.py
@@ -9,6 +9,7 @@
 
 BLK = 128
 LANES = 128
+WIDE = 256
 F32 = jnp.float32
 BF16 = jnp.bfloat16
 MESH = pl.DeviceIdType.MESH
@@ -19,36 +20,57 @@
     return high, (values - high.astype(F32)).astype(BF16)
 
 
-def low_hot(index):
-    rows = lax.broadcasted_iota(jnp.int32, (LANES, index.shape[1]), 0)
-    return jnp.where(rows == (index & (LANES - 1)), 1.0, 0.0).astype(BF16)
-
-
-def high_mask(index, rows):
-    return lax.broadcasted_iota(jnp.int32, (rows, index.shape[1]), 0) == (index >> 7)
-
-
-def picked(table, rows, index):
-    hot = low_hot(index)
-    wide = jnp.dot(table, jnp.concatenate([hot, hot], axis=0), preferred_element_type=F32)
-    mask = high_mask(index, rows)
-    return [jnp.where(mask, wide[c * rows : (c + 1) * rows], 0.0) for c in range(3)]
-
-
-def spread(values, index, rows):
-    mask = high_mask(index, rows)
+def hot(index, count):
+    rows = lax.broadcasted_iota(jnp.int32, (count, index.shape[1]), 0)
+    return jnp.where(rows == (index & (count - 1)), 1.0, 0.0).astype(BF16)
+
+
+def row_of(index, heights):
+    inside = (index >= 0) & (index < heights * WIDE)
+    return jnp.where(inside, (index >> 8) + heights * ((index >> 7) & 1), -1)
+
+
+def picked(table, heights, index):
+    rows = 2 * heights
+    low = hot(index, LANES)
+    wide = jnp.dot(table, jnp.concatenate([low, low], axis=0), preferred_element_type=F32)
+    row = row_of(index, heights)
+    eight = lax.broadcasted_iota(jnp.int32, (8, index.shape[1]), 0)
+    sums = [None] * 3
+    for g in range(0, rows, 8):
+        mask = eight + g == row
+        for c in range(3):
+            term = jnp.where(mask, wide[c * rows + g : c * rows + g + 8], 0.0)
+            sums[c] = term if sums[c] is None else sums[c] + term
+    return sums
+
+
+def chunked(table, heights, index):
+    parts = [picked(table, heights, index[:, e : e + WIDE]) for e in range(0, index.shape[1], WIDE)]
+    return [jnp.concatenate([p[c] for p in parts], axis=1) for c in range(3)]
+
+
+def spread(values, index, heights):
+    mask = lax.broadcasted_iota(jnp.int32, (heights, index.shape[1]), 0) == (index >> 8)
     pieces = [split(v) for v in values]
     blocks = []
     for p in range(2):
         for c in range(3):
             piece = jnp.broadcast_to(pieces[c][p].astype(F32), mask.shape)
-            blocks.append(jnp.where(mask, piece, 0.0).astype(BF16))
+            blocks.append(jnp.where(mask, piece, 0.0))
     return lax.dot_general(
-        jnp.concatenate(blocks, axis=0),
-        low_hot(index),
+        jnp.concatenate(blocks, axis=0).astype(BF16),
+        hot(index, WIDE),
         (((1,), (1,)), ((), ())),
         preferred_element_type=F32,
     )
+
+
+def store_table(table, full, rows):
+    for c in range(3):
+        high, low = split(full[c])
+        table[c * rows : (c + 1) * rows, :LANES] = high
+        table[c * rows : (c + 1) * rows, LANES:] = low
 
 
 def kernel(
@@ -68,14 +90,26 @@
     send_nodes,
     send_count,
     ref_stiff,
-    iterate_next,
-    residual_next,
-    direction_next,
-    table_f,
-    table,
+    result,
+    background_v,
+    obs_weight_v,
+    connect_v,
+    elem_scale_v,
+    reg_weight_v,
+    iterate_v,
+    residual_v,
+    direction_v,
+    send_nodes_v,
+    send_count_v,
+    ref_stiff_v,
+    own_f,
+    ghost_f,
+    own_table,
+    ghost_table,
     state,
     coupled,
     acc,
+    ghost_acc,
     own,
     own_in,
     out_a,
@@ -86,18 +120,45 @@
     ret_in,
     red,
     red_in,
+    sems_in,
     sems_a,
     sems_b,
     sems_r,
     sems_x,
     sems_s,
 ):
+    loads = {}
+    given = dict(
+        background=(background, background_v),
+        send_nodes=(send_nodes, send_nodes_v),
+        send_count=(send_count, send_count_v),
+        connect=(connect, connect_v),
+        direction=(direction, direction_v),
+        elem_scale=(elem_scale, elem_scale_v),
+        ref_stiff=(ref_stiff, ref_stiff_v),
+        obs_weight=(obs_weight, obs_weight_v),
+        reg_weight=(reg_weight, reg_weight_v),
+        residual=(residual, residual_v),
+        iterate=(iterate, iterate_v),
+    )
+    for i, (name, (source, target)) in enumerate(given.items()):
+        loads[name] = pltpu.make_async_copy(source, target, sems_in.at[i])
+        loads[name].start()
+    background, obs_weight, connect = background_v, obs_weight_v, connect_v
+    elem_scale, reg_weight, iterate, residual = elem_scale_v, reg_weight_v, iterate_v, residual_v
+    direction, send_nodes, send_count, ref_stiff = direction_v, send_nodes_v, send_count_v, ref_stiff_v
+
+    def arrive(*names):
+        for name in names:
+            loads[name].wait()
+
     d, s, f = (lax.axis_index(a) for a in ("dom", "sub", "field"))
     elements = connect.shape[1]
     link = send_nodes.shape[3]
-    own_rows = obs_weight.shape[0]
-    rows = table_f.shape[1]
-    per_link = link // LANES
+    own_high = own_f.shape[1] // 2
+    ghost_high = ghost_f.shape[1] // 2
+    owned = own_high * WIDE
+    per_link = link // WIDE
     links = [(o, t) for o in range(3) for t in range(subs) if (o, t) != (1, 0)]
 
     def at(dd, ds, df):
@@ -127,23 +188,21 @@
     for offset in greeted:
         pl.semaphore_signal(barrier, inc=1, device_id=at(*offset), device_id_type=MESH)
 
-    table_f[...] = jnp.zeros_like(table_f)
-    for r in range(own_rows):
-        table_f[:, r, :] = background[:, r * LANES : (r + 1) * LANES]
-
-    def fill_table(part):
-        for c in range(3):
-            high, low = split(table_f[c])
-            table[c * rows : (c + 1) * rows, :LANES] = high
-            table[c * rows : (c + 1) * rows, LANES:] = low
+    ghost_f[...] = jnp.zeros_like(ghost_f)
+    arrive("background", "send_nodes", "send_count")
+    for h in range(own_high):
+        for half in range(2):
+            r = (2 * h + half) * LANES
+            own_f[:, half * own_high + h, :] = background[:, r : r + LANES]
+    store_table(own_table, own_f, 2 * own_high)
 
     def outbound(out):
         for o in range(3):
             for t in range(subs):
                 index = send_nodes[0, o, t : t + 1, :]
                 slot = lax.broadcasted_iota(jnp.int32, index.shape, 1)
-                open_slot = jnp.where(slot < send_count[0, o, t], 1.0, 0.0)
-                for c, wide in enumerate(picked(table[...], rows, index)):
+                open_slot = jnp.where(slot < send_count[0, t, o], 1.0, 0.0)
+                for c, wide in enumerate(picked(own_table[...], own_high, index)):
                     out[o * subs + t, c : c + 1, :] = open_slot * jnp.sum(wide, axis=0, keepdims=True)
 
     def ghost_copy(o, t, out, landing, sems):
@@ -166,25 +225,27 @@
             device_id_type=MESH,
         )
 
-    def exchange(out, landing, sems):
+    def exchange_start(out, landing, sems):
         for o, t in links:
             when(o, lambda o=o, t=t: ghost_copy(o, t, out, landing, sems).start())
+
+    def exchange_end(out, landing, sems):
         for o, t in links:
             when(o, lambda o=o, t=t: ghost_arrival(o, t, out, landing, sems).wait_recv())
-        for o, t in links:
-            when(o, lambda o=o, t=t: ghost_copy(o, t, out, landing, sems).wait_send())
 
     def ghosts_in(landing):
         for q in range(3 * subs):
             for h in range(per_link):
-                table_f[:, own_rows + q * per_link + h, :] = landing[q, :, h * LANES : (h + 1) * LANES]
-
-    fill_table(0)
+                for half in range(2):
+                    e = (2 * h + half) * LANES
+                    ghost_f[:, half * ghost_high + q * per_link + h, :] = landing[q, :, e : e + LANES]
+        store_table(ghost_table, ghost_f, 2 * ghost_high)
+
     outbound(out_a)
     pl.semaphore_wait(barrier, len(greeted))
-    exchange(out_a, in_a, sems_a)
-    ghosts_in(in_a)
-    fill_table(1)
+    exchange_start(out_a, in_a, sems_a)
+    arrive("connect", "direction", "elem_scale", "ref_stiff", "obs_weight")
+    arrive("reg_weight", "residual", "iterate")
 
     element = lax.broadcasted_iota(jnp.int32, (1, elements), 1)
     live = jnp.where(element < BLK * live_blocks[0], 1.0, 0.0)
@@ -195,31 +256,47 @@
 
     def pull(k, carry):
         index = connect[pl.ds(k, 1), :]
-        for c, wide in enumerate(picked(table[...], rows, index)):
+        for c, wide in enumerate(chunked(own_table[...], own_high, index)):
             state[pl.ds(c * nodes + k, 1), :] = jnp.sum(wide, axis=0, keepdims=True)
         return carry
 
+    def pull_ghosts(k, carry):
+        index = connect[pl.ds(k, 1), :] - owned
+        for c, wide in enumerate(chunked(ghost_table[...], ghost_high, index)):
+            state[pl.ds(c * nodes + k, 1), :] += jnp.sum(wide, axis=0, keepdims=True)
+        return carry
+
     lax.fori_loop(0, nodes, pull, 0)
+    exchange_end(out_a, in_a, sems_a)
+    ghosts_in(in_a)
+    lax.fori_loop(0, nodes, pull_ghosts, 0)
     coupled[...] = (live * elem_scale[...]) * jnp.dot(
         ref_stiff[...], state[...], precision=lax.Precision.HIGHEST, preferred_element_type=F32
     )
 
     acc[...] = jnp.zeros_like(acc)
+    ghost_acc[...] = jnp.zeros_like(ghost_acc)
+
+    def push_ghosts(k, carry):
+        index = connect[pl.ds(k, 1), :] - owned
+        terms = [search * coupled[pl.ds(c * nodes + k, 1), :] for c in range(3)]
+        ghost_acc[...] += spread(terms, index, ghost_high)
+        return carry
 
     def push(k, carry):
         index = connect[pl.ds(k, 1), :]
         terms = [search * coupled[pl.ds(c * nodes + k, 1), :] for c in range(3)]
-        acc[...] += spread(terms, index, rows)
+        acc[...] += spread(terms, index, own_high)
         return carry
 
-    lax.fori_loop(0, nodes, push, 0)
+    lax.fori_loop(0, nodes, push_ghosts, 0)
     for c in range(3):
-        total = acc[c * rows : (c + 1) * rows, :] + acc[(3 + c) * rows : (4 + c) * rows, :]
-        own[c] = total[:own_rows]
+        total = ghost_acc[c * ghost_high : (c + 1) * ghost_high, :]
+        total = total + ghost_acc[(3 + c) * ghost_high : (4 + c) * ghost_high, :]
         for q in range(3 * subs):
             for h in range(per_link):
-                r = own_rows + q * per_link + h
-                ret[q, c : c + 1, h * LANES : (h + 1) * LANES] = total[r : r + 1]
+                r = q * per_link + h
+                ret[q, c : c + 1, h * WIDE : (h + 1) * WIDE] = total[r : r + 1]
 
     def ret_copy(o, t, g):
         return pltpu.make_async_remote_copy(
@@ -254,6 +331,9 @@
     for o, t in links:
         for g in range(fields):
             when(o, lambda o=o, t=t, g=g: ret_copy(o, t, g).start())
+    lax.fori_loop(0, nodes, push, 0)
+    for c in range(3):
+        own[c] = acc[c * own_high : (c + 1) * own_high, :] + acc[(3 + c) * own_high : (4 + c) * own_high, :]
     for g in range(1, fields):
         own_copy(g).start()
     for o, t in links:
@@ -265,11 +345,11 @@
             q = o * subs + t
             index = send_nodes[0, o, t : t + 1, :]
             slot = lax.broadcasted_iota(jnp.int32, index.shape, 1)
-            open_slot = jnp.where(slot < send_count[0, o, t], 1.0, 0.0)
+            open_slot = jnp.where(slot < send_count[0, t, o], 1.0, 0.0)
             sums = ret_in[0, q]
             for g in range(1, fields):
                 sums = sums + ret_in[g, q]
-            part = spread([open_slot * sums[c : c + 1] for c in range(3)], index, own_rows)
+            part = spread([open_slot * sums[c : c + 1] for c in range(3)], index, own_high)
             landed = part if landed is None else landed + part
     for g in range(1, fields):
         own_copy(g).wait_recv()
@@ -277,23 +357,31 @@
         assembled = own[c]
         for g in range(1, fields):
             assembled = assembled + own_in[g - 1, c]
-        assembled = assembled + landed[c * own_rows : (c + 1) * own_rows]
-        assembled = assembled + landed[(3 + c) * own_rows : (4 + c) * own_rows]
-        table_f[c, :own_rows, :] = obs_weight[...] * assembled
-
-    fill_table(0)
+        assembled = assembled + landed[c * own_high : (c + 1) * own_high]
+        assembled = assembled + landed[(3 + c) * own_high : (4 + c) * own_high]
+        for half in range(2):
+            weight = obs_weight[pl.ds(half, own_high, stride=2), :]
+            part = assembled[:, half * LANES : (half + 1) * LANES]
+            own_f[c, half * own_high : (half + 1) * own_high, :] = weight * part
+
+    store_table(own_table, own_f, 2 * own_high)
     outbound(out_b)
-    exchange(out_b, in_b, sems_b)
+    exchange_start(out_b, in_b, sems_b)
+
+    def back(table, heights, base):
+        def step(k, total):
+            index = connect[pl.ds(k, 1), :] - base
+            for c, wide in enumerate(chunked(table[...], heights, index)):
+                total = total + coupled[pl.ds(c * nodes + k, 1), :] * wide
+            return total
+
+        return step
+
+    hess8 = lax.fori_loop(0, nodes, back(own_table, own_high, 0), jnp.zeros((8, elements), F32))
+    exchange_end(out_b, in_b, sems_b)
     ghosts_in(in_b)
-    fill_table(1)
-
-    def back(k, total):
-        index = connect[pl.ds(k, 1), :]
-        for c, wide in enumerate(picked(table[...], rows, index)):
-            total = total + coupled[pl.ds(c * nodes + k, 1), :] * jnp.sum(wide, axis=0, keepdims=True)
-        return total
-
-    hess = lax.fori_loop(0, nodes, back, jnp.zeros((1, elements), F32)) + reg_weight[...] * search
+    hess8 = lax.fori_loop(0, nodes, back(ghost_table, ghost_high, owned), hess8)
+    hess = jnp.sum(hess8, axis=0, keepdims=True) + reg_weight[...] * search
 
     def lane_sums(values):
         total = values[:, :LANES]
@@ -334,14 +422,31 @@
     step = before / curvature
     after = before - 2.0 * step * cross + step * step * image
     remain_next = remain - step * hess
-    iterate_next[...] = guess + step * search
-    residual_next[...] = remain_next
-    direction_next[...] = remain_next + (after / before) * search
+    result[0] = guess + step * search
+    result[1] = remain_next
+    result[2] = remain_next + (after / before) * search
+    for out, landing, sems in ((out_a, in_a, sems_a), (out_b, in_b, sems_b)):
+        for o, t in links:
+            when(
+                o,
+                lambda o=o, t=t, out=out, landing=landing, sems=sems: ghost_copy(
+                    o, t, out, landing, sems
+                ).wait_send(),
+            )
     for o, t in links:
         for g in range(fields):
             when(o, lambda o=o, t=t, g=g: ret_copy(o, t, g).wait_send())
     for g in range(1, fields):
         own_copy(g).wait_send()
+
+
+def hand_out(result, iterate_next, residual_next, direction_next, sems):
+    outs = (iterate_next, residual_next, direction_next)
+    copies = [pltpu.make_async_copy(result.at[i], outs[i], sems.at[i]) for i in range(3)]
+    for copy in copies:
+        copy.start()
+    for copy in copies:
+        copy.wait()
 
 
 def solution(mesh):
@@ -369,25 +474,47 @@
     ):
         elements = connect.shape[1]
         link = send_nodes.shape[3]
-        own_rows = background.shape[1] // LANES
         links = 3 * subs
-        rows = -(-(own_rows + links * link // LANES) // 16) * 16
+        nodes = connect.shape[0]
+        own_high = background.shape[1] // WIDE
+        ghost_high = -(-links * link // WIDE // 8) * 8
         vmem = pl.BlockSpec(memory_space=pltpu.VMEM)
         smem = pl.BlockSpec(memory_space=pltpu.SMEM)
+        hbm = pl.BlockSpec(memory_space=pltpu.HBM)
         partners = sum(len(stage) for stage in stages)
-        outs = pl.pallas_call(
+        row = (1, elements)
+        operands = (
+            background,
+            obs_weight.reshape(-1, LANES),
+            connect,
+            live_blocks,
+            elem_scale.reshape(row),
+            reg_weight.reshape(row),
+            iterate.reshape(row),
+            residual.reshape(row),
+            direction.reshape(row),
+            send_nodes,
+            send_count.transpose(0, 2, 1),
+            ref_stiff,
+        )
+        spaces = [pltpu.VMEM] * 9 + [pltpu.SMEM, pltpu.VMEM]
+        result = pl.pallas_call(
             functools.partial(kernel, doms, subs, fields, stages),
-            out_shape=[jax.ShapeDtypeStruct((1, elements), F32)] * 3,
-            in_specs=[vmem, vmem, vmem, smem, vmem, vmem, vmem, vmem, vmem, vmem, smem, vmem],
-            out_specs=[vmem] * 3,
-            scratch_shapes=[
-                pltpu.VMEM((3, rows, LANES), F32),
-                pltpu.VMEM((3 * rows, 2 * LANES), BF16),
-                pltpu.VMEM((3 * connect.shape[0], elements), F32),
-                pltpu.VMEM((3 * connect.shape[0], elements), F32),
-                pltpu.VMEM((6 * rows, LANES), F32),
-                pltpu.VMEM((3, own_rows, LANES), F32),
-                pltpu.VMEM((max(fields - 1, 1), 3, own_rows, LANES), F32),
+            out_shape=jax.ShapeDtypeStruct((3,) + row, F32),
+            in_specs=[hbm] * 3 + [smem] + [hbm] * 8,
+            out_specs=vmem,
+            scratch_shapes=[space(x.shape, x.dtype) for space, x in zip(spaces, operands[:3] + operands[4:])]
+            + [
+                pltpu.VMEM((3, 2 * own_high, LANES), F32),
+                pltpu.VMEM((3, 2 * ghost_high, LANES), F32),
+                pltpu.VMEM((6 * own_high, WIDE), BF16),
+                pltpu.VMEM((6 * ghost_high, WIDE), BF16),
+                pltpu.VMEM((3 * nodes, elements), F32),
+                pltpu.VMEM((3 * nodes, elements), F32),
+                pltpu.VMEM((6 * own_high, WIDE), F32),
+                pltpu.VMEM((6 * ghost_high, WIDE), F32),
+                pltpu.VMEM((3, own_high, WIDE), F32),
+                pltpu.VMEM((max(fields - 1, 1), 3, own_high, WIDE), F32),
                 pltpu.VMEM((links, 3, link), F32),
                 pltpu.VMEM((links, 3, link), F32),
                 pltpu.VMEM((links, 3, link), F32),
@@ -396,6 +523,7 @@
                 pltpu.VMEM((fields, links, 3, link), F32),
                 pltpu.VMEM((len(stages) + 1, 8, LANES), F32),
                 pltpu.VMEM((partners, 8, LANES), F32),
+                pltpu.SemaphoreType.DMA((11,)),
                 pltpu.SemaphoreType.DMA((2, links)),
                 pltpu.SemaphoreType.DMA((2, links)),
                 pltpu.SemaphoreType.DMA((2, fields, links)),
@@ -403,22 +531,16 @@
                 pltpu.SemaphoreType.DMA((2, partners)),
             ],
             compiler_params=pltpu.CompilerParams(
-                collective_id=0, has_side_effects=True, vmem_limit_bytes=48 * 1024 * 1024
+                collective_id=0, has_side_effects=True, vmem_limit_bytes=67043328
             ),
-        )(
-            background,
-            obs_weight.reshape(own_rows, LANES),
-            connect,
-            live_blocks,
-            elem_scale.reshape(1, elements),
-            reg_weight.reshape(1, elements),
-            iterate.reshape(1, elements),
-            residual.reshape(1, elements),
-            direction.reshape(1, elements),
-            send_nodes,
-            send_count,
-            ref_stiff,
-        )
+        )(*operands)
+        outs = pl.pallas_call(
+            hand_out,
+            out_shape=[jax.ShapeDtypeStruct(row, F32)] * 3,
+            in_specs=[vmem],
+            out_specs=[hbm] * 3,
+            scratch_shapes=[pltpu.SemaphoreType.DMA((3,))],
+        )(result)
         return tuple(x.reshape(elements) for x in outs)
 
     owned = P(("groups", "dom", "sub"))

time: 42.2 us -> 33 us (0.78)
  local copies, waits for them, and re-layouts: 9.07 us -> 0 us
    unnamed x24 -> x0, local copies, waits for them, and re-layouts: 9.07 us -> none
    pallas_call x0 -> x1, Pallas kernels: none -> 1.33 us  [on_device(): pl.pallas_call(hand_out, out_shape=[jax.ShapeDtypeStruct(row, F32)] * 3,...]
    pallas_call x1, Pallas kernels: 31.3 us -> 30.1 us  [on_device(): pl.pallas_call(functools.partial(kernel, doms, subs, fields, stages), out...]
where the time goes in v2:
time: 33 us; the launch traced here: 32.7 us
  Pallas kernels  31.4 us (95%)
  between operations  1.29 us (4%)
    pallas_call x1, Pallas kernels, on_device(): pl.pallas_call(functools.partial(kernel, doms, subs, fields, stages), out...  30.1 us
    pallas_call x1, Pallas kernels, on_device(): pl.pallas_call(hand_out, out_shape=[jax.ShapeDtypeStruct(row, F32)] * 3,...  1.33 us

profile of v2, /device:TPU:0, one launch (start us, length us, event | category | flops | bytes accessed | tf_op | source)
XLA Modules:
  0.0 32.7 jit_solution(14422313251596360783)
XLA Ops:
  1.3 30.1 %shard_map.139.result = f32[3,1,1024]{2,1,0:T(1,128)} custom-call(f32[3,4096]{1,0:T(4,128)} %background.1, f32[32,128]{1,0:T(8,128)} %bitcast.10, s32[10,1024]{1,0:T(8,128)} %connect.1, s32[1]{0:T(128)S(6)} %copy.15.live_blocks, f32[1,1024]{1,0:T(1,128)} %bitcast.11, f32[1,1024]{1,0:T(1,128)} %bitcast.12, f32[1,1024]{1,0:T(1,128)} %bitcast.13, ...), custom_call_target="tpu_custom_call" | custom-call | tf_op jit(solution)/shard_map/pallas_call | solution.py:501
  31.4 1.3 %shard_map.140 = (f32[1,1024]{1,0:T(1,128)}, f32[1,1024]{1,0:T(1,128)}, f32[1,1024]{1,0:T(1,128)}) custom-call(f32[3,1,1024]{2,1,0:T(1,128)} %shard_map.139.result), custom_call_target="tpu_custom_call" | custom-call | tf_op jit(solution)/shard_map/pallas_call | solution.py:537

commit v3 on v2

--- a/solution.py
+++ b/solution.py
@@ -25,33 +25,27 @@
     return jnp.where(rows == (index & (count - 1)), 1.0, 0.0).astype(BF16)
 
 
-def row_of(index, heights):
-    inside = (index >= 0) & (index < heights * WIDE)
-    return jnp.where(inside, (index >> 8) + heights * ((index >> 7) & 1), -1)
-
-
-def picked(table, heights, index):
-    rows = 2 * heights
-    low = hot(index, LANES)
-    wide = jnp.dot(table, jnp.concatenate([low, low], axis=0), preferred_element_type=F32)
-    row = row_of(index, heights)
+def picked(table, rows, index):
+    wide = jnp.dot(table, hot(index, LANES), preferred_element_type=F32)
+    row = index >> 7
     eight = lax.broadcasted_iota(jnp.int32, (8, index.shape[1]), 0)
     sums = [None] * 3
     for g in range(0, rows, 8):
         mask = eight + g == row
         for c in range(3):
-            term = jnp.where(mask, wide[c * rows + g : c * rows + g + 8], 0.0)
+            high, low = c * rows + g, (3 + c) * rows + g
+            term = jnp.where(mask, wide[high : high + 8] + wide[low : low + 8], 0.0)
             sums[c] = term if sums[c] is None else sums[c] + term
     return sums
 
 
-def chunked(table, heights, index):
-    parts = [picked(table, heights, index[:, e : e + WIDE]) for e in range(0, index.shape[1], WIDE)]
+def chunked(table, rows, index):
+    parts = [picked(table, rows, index[:, e : e + WIDE]) for e in range(0, index.shape[1], WIDE)]
     return [jnp.concatenate([p[c] for p in parts], axis=1) for c in range(3)]
 
 
 def spread(values, index, heights):
-    mask = lax.broadcasted_iota(jnp.int32, (heights, index.shape[1]), 0) == (index >> 8)
+    mask = lax.broadcasted_iota(jnp.int32, (heights, index.shape[1]), 0) == (index >> 7)
     pieces = [split(v) for v in values]
     blocks = []
     for p in range(2):
@@ -60,7 +54,7 @@
             blocks.append(jnp.where(mask, piece, 0.0))
     return lax.dot_general(
         jnp.concatenate(blocks, axis=0).astype(BF16),
-        hot(index, WIDE),
+        hot(index, LANES),
         (((1,), (1,)), ((), ())),
         preferred_element_type=F32,
     )
@@ -69,8 +63,8 @@
 def store_table(table, full, rows):
     for c in range(3):
         high, low = split(full[c])
-        table[c * rows : (c + 1) * rows, :LANES] = high
-        table[c * rows : (c + 1) * rows, LANES:] = low
+        table[c * rows : (c + 1) * rows, :] = high
+        table[(3 + c) * rows : (4 + c) * rows, :] = low
 
 
 def kernel(
@@ -155,10 +149,10 @@
     d, s, f = (lax.axis_index(a) for a in ("dom", "sub", "field"))
     elements = connect.shape[1]
     link = send_nodes.shape[3]
-    own_high = own_f.shape[1] // 2
-    ghost_high = ghost_f.shape[1] // 2
-    owned = own_high * WIDE
-    per_link = link // WIDE
+    own_high = own_f.shape[1]
+    ghost_high = ghost_f.shape[1]
+    owned = own_high * LANES
+    per_link = link // LANES
     links = [(o, t) for o in range(3) for t in range(subs) if (o, t) != (1, 0)]
 
     def at(dd, ds, df):
@@ -191,19 +185,20 @@
     ghost_f[...] = jnp.zeros_like(ghost_f)
     arrive("background", "send_nodes", "send_count")
     for h in range(own_high):
-        for half in range(2):
-            r = (2 * h + half) * LANES
-            own_f[:, half * own_high + h, :] = background[:, r : r + LANES]
-    store_table(own_table, own_f, 2 * own_high)
+        own_f[:, h, :] = background[:, h * LANES : (h + 1) * LANES]
+    store_table(own_table, own_f, own_high)
+
+    def link_index(o, t):
+        other = lax.rem(s + t, subs)
+        index = send_nodes[0, o, pl.ds(other, 1), :]
+        slot = lax.broadcasted_iota(jnp.int32, index.shape, 1)
+        return index, jnp.where(slot < send_count[0, other, o], 1.0, 0.0), o * subs + other
 
     def outbound(out):
-        for o in range(3):
-            for t in range(subs):
-                index = send_nodes[0, o, t : t + 1, :]
-                slot = lax.broadcasted_iota(jnp.int32, index.shape, 1)
-                open_slot = jnp.where(slot < send_count[0, t, o], 1.0, 0.0)
-                for c, wide in enumerate(picked(own_table[...], own_high, index)):
-                    out[o * subs + t, c : c + 1, :] = open_slot * jnp.sum(wide, axis=0, keepdims=True)
+        for o, t in links:
+            index, open_slot, q = link_index(o, t)
+            for c, wide in enumerate(picked(own_table[...], own_high, index)):
+                out[q, c : c + 1, :] = open_slot * jnp.sum(wide, axis=0, keepdims=True)
 
     def ghost_copy(o, t, out, landing, sems):
         return pltpu.make_async_remote_copy(
@@ -236,10 +231,8 @@
     def ghosts_in(landing):
         for q in range(3 * subs):
             for h in range(per_link):
-                for half in range(2):
-                    e = (2 * h + half) * LANES
-                    ghost_f[:, half * ghost_high + q * per_link + h, :] = landing[q, :, e : e + LANES]
-        store_table(ghost_table, ghost_f, 2 * ghost_high)
+                ghost_f[:, q * per_link + h, :] = landing[q, :, h * LANES : (h + 1) * LANES]
+        store_table(ghost_table, ghost_f, ghost_high)
 
     outbound(out_a)
     pl.semaphore_wait(barrier, len(greeted))
@@ -296,7 +289,7 @@
         for q in range(3 * subs):
             for h in range(per_link):
                 r = q * per_link + h
-                ret[q, c : c + 1, h * WIDE : (h + 1) * WIDE] = total[r : r + 1]
+                ret[q, c : c + 1, h * LANES : (h + 1) * LANES] = total[r : r + 1]
 
     def ret_copy(o, t, g):
         return pltpu.make_async_remote_copy(
@@ -340,17 +333,13 @@
         for g in range(fields):
             when(o, lambda o=o, t=t, g=g: ret_arrival(o, t, g).wait_recv())
     landed = None
-    for o in range(3):
-        for t in range(subs):
-            q = o * subs + t
-            index = send_nodes[0, o, t : t + 1, :]
-            slot = lax.broadcasted_iota(jnp.int32, index.shape, 1)
-            open_slot = jnp.where(slot < send_count[0, t, o], 1.0, 0.0)
-            sums = ret_in[0, q]
-            for g in range(1, fields):
-                sums = sums + ret_in[g, q]
-            part = spread([open_slot * sums[c : c + 1] for c in range(3)], index, own_high)
-            landed = part if landed is None else landed + part
+    for o, t in links:
+        index, open_slot, q = link_index(o, t)
+        sums = ret_in[0, q]
+        for g in range(1, fields):
+            sums = sums + ret_in[g, q]
+        part = spread([open_slot * sums[c : c + 1] for c in range(3)], index, own_high)
+        landed = part if landed is None else landed + part
     for g in range(1, fields):
         own_copy(g).wait_recv()
     for c in range(3):
@@ -359,12 +348,9 @@
             assembled = assembled + own_in[g - 1, c]
         assembled = assembled + landed[c * own_high : (c + 1) * own_high]
         assembled = assembled + landed[(3 + c) * own_high : (4 + c) * own_high]
-        for half in range(2):
-            weight = obs_weight[pl.ds(half, own_high, stride=2), :]
-            part = assembled[:, half * LANES : (half + 1) * LANES]
-            own_f[c, half * own_high : (half + 1) * own_high, :] = weight * part
-
-    store_table(own_table, own_f, 2 * own_high)
+        own_f[c] = obs_weight[...] * assembled
+
+    store_table(own_table, own_f, own_high)
     outbound(out_b)
     exchange_start(out_b, in_b, sems_b)
 
@@ -476,8 +462,8 @@
         link = send_nodes.shape[3]
         links = 3 * subs
         nodes = connect.shape[0]
-        own_high = background.shape[1] // WIDE
-        ghost_high = -(-links * link // WIDE // 8) * 8
+        own_high = background.shape[1] // LANES
+        ghost_high = -(-links * link // LANES // 16) * 16
         vmem = pl.BlockSpec(memory_space=pltpu.VMEM)
         smem = pl.BlockSpec(memory_space=pltpu.SMEM)
         hbm = pl.BlockSpec(memory_space=pltpu.HBM)
@@ -505,16 +491,16 @@
             out_specs=vmem,
             scratch_shapes=[space(x.shape, x.dtype) for space, x in zip(spaces, operands[:3] + operands[4:])]
             + [
-                pltpu.VMEM((3, 2 * own_high, LANES), F32),
-                pltpu.VMEM((3, 2 * ghost_high, LANES), F32),
-                pltpu.VMEM((6 * own_high, WIDE), BF16),
-                pltpu.VMEM((6 * ghost_high, WIDE), BF16),
+                pltpu.VMEM((3, own_high, LANES), F32),
+                pltpu.VMEM((3, ghost_high, LANES), F32),
+                pltpu.VMEM((6 * own_high, LANES), BF16),
+                pltpu.VMEM((6 * ghost_high, LANES), BF16),
                 pltpu.VMEM((3 * nodes, elements), F32),
                 pltpu.VMEM((3 * nodes, elements), F32),
-                pltpu.VMEM((6 * own_high, WIDE), F32),
-                pltpu.VMEM((6 * ghost_high, WIDE), F32),
-                pltpu.VMEM((3, own_high, WIDE), F32),
-                pltpu.VMEM((max(fields - 1, 1), 3, own_high, WIDE), F32),
+                pltpu.VMEM((6 * own_high, LANES), F32),
+                pltpu.VMEM((6 * ghost_high, LANES), F32),
+                pltpu.VMEM((3, own_high, LANES), F32),
+                pltpu.VMEM((max(fields - 1, 1), 3, own_high, LANES), F32),
                 pltpu.VMEM((links, 3, link), F32),
                 pltpu.VMEM((links, 3, link), F32),
                 pltpu.VMEM((links, 3, link), F32),

time: 33 us -> 31.9 us (0.967)
  Pallas kernels: 31.4 us -> 30.4 us
    pallas_call x1, Pallas kernels: 30.1 us -> 29 us  [on_device(): pl.pallas_call(functools.partial(kernel, doms, subs, fields, stages), out...]
where the time goes in v3:
time: 31.9 us; the launch traced here: 31.7 us
  Pallas kernels  30.4 us (95%)
  between operations  1.29 us (4%)
    pallas_call x1, Pallas kernels, on_device(): pl.pallas_call(functools.partial(kernel, doms, subs, fields, stages), out...  29 us
    pallas_call x1, Pallas kernels, on_device(): pl.pallas_call(hand_out, out_shape=[jax.ShapeDtypeStruct(row, F32)] * 3,...  1.33 us

profile of v3, /device:TPU:0, one launch (start us, length us, event | category | flops | bytes accessed | tf_op | source)
XLA Modules:
  0.0 31.7 jit_solution(8292015832051130799)
XLA Ops:
  1.3 29.0 %shard_map.139.result = f32[3,1,1024]{2,1,0:T(1,128)} custom-call(f32[3,4096]{1,0:T(4,128)} %background.1, f32[32,128]{1,0:T(8,128)} %bitcast.10, s32[10,1024]{1,0:T(8,128)} %connect.1, s32[1]{0:T(128)S(6)} %copy.15.live_blocks, f32[1,1024]{1,0:T(1,128)} %bitcast.11, f32[1,1024]{1,0:T(1,128)} %bitcast.12, f32[1,1024]{1,0:T(1,128)} %bitcast.13, ...), custom_call_target="tpu_custom_call" | custom-call | tf_op jit(solution)/shard_map/pallas_call | solution.py:487
  30.3 1.3 %shard_map.140 = (f32[1,1024]{1,0:T(1,128)}, f32[1,1024]{1,0:T(1,128)}, f32[1,1024]{1,0:T(1,128)}) custom-call(f32[3,1,1024]{2,1,0:T(1,128)} %shard_map.139.result), custom_call_target="tpu_custom_call" | custom-call | tf_op jit(solution)/shard_map/pallas_call | solution.py:523

commit v4 on v3

--- a/solution.py
+++ b/solution.py
@@ -8,6 +8,7 @@
 from jax.sharding import PartitionSpec as P
 
 BLK = 128
+UNROLL = 2
 LANES = 128
 WIDE = 256
 F32 = jnp.float32
@@ -45,19 +46,32 @@
 
 
 def spread(values, index, heights):
-    mask = lax.broadcasted_iota(jnp.int32, (heights, index.shape[1]), 0) == (index >> 7)
-    pieces = [split(v) for v in values]
+    row = jnp.broadcast_to(index >> 7, (16, index.shape[1])).astype(jnp.int16)
+    place = lax.broadcasted_iota(jnp.int32, (16, index.shape[1]), 0).astype(jnp.int16)
+    pieces = [split(jnp.broadcast_to(v, (16, v.shape[1]))) for v in values]
+    zero = jnp.zeros(row.shape, BF16)
     blocks = []
     for p in range(2):
         for c in range(3):
-            piece = jnp.broadcast_to(pieces[c][p].astype(F32), mask.shape)
-            blocks.append(jnp.where(mask, piece, 0.0))
+            for g in range(0, heights, 16):
+                blocks.append(jnp.where(place + jnp.int16(g) == row, pieces[c][p], zero))
     return lax.dot_general(
-        jnp.concatenate(blocks, axis=0).astype(BF16),
+        jnp.concatenate(blocks, axis=0),
         hot(index, LANES),
         (((1,), (1,)), ((), ())),
         preferred_element_type=F32,
     )
+
+
+def each(count, step, carry):
+    by = next(u for u in (UNROLL, 1) if count % u == 0)
+
+    def trip(i, carry):
+        for j in range(by):
+            carry = step(i * by + j, carry)
+        return carry
+
+    return lax.fori_loop(0, count // by, trip, carry)
 
 
 def store_table(table, full, rows):
@@ -259,10 +273,10 @@
             state[pl.ds(c * nodes + k, 1), :] += jnp.sum(wide, axis=0, keepdims=True)
         return carry
 
-    lax.fori_loop(0, nodes, pull, 0)
+    each(nodes, pull, 0)
     exchange_end(out_a, in_a, sems_a)
     ghosts_in(in_a)
-    lax.fori_loop(0, nodes, pull_ghosts, 0)
+    each(nodes, pull_ghosts, 0)
     coupled[...] = (live * elem_scale[...]) * jnp.dot(
         ref_stiff[...], state[...], precision=lax.Precision.HIGHEST, preferred_element_type=F32
     )
@@ -282,7 +296,7 @@
         acc[...] += spread(terms, index, own_high)
         return carry
 
-    lax.fori_loop(0, nodes, push_ghosts, 0)
+    each(nodes, push_ghosts, 0)
     for c in range(3):
         total = ghost_acc[c * ghost_high : (c + 1) * ghost_high, :]
         total = total + ghost_acc[(3 + c) * ghost_high : (4 + c) * ghost_high, :]
@@ -324,7 +338,7 @@
     for o, t in links:
         for g in range(fields):
             when(o, lambda o=o, t=t, g=g: ret_copy(o, t, g).start())
-    lax.fori_loop(0, nodes, push, 0)
+    each(nodes, push, 0)
     for c in range(3):
         own[c] = acc[c * own_high : (c + 1) * own_high, :] + acc[(3 + c) * own_high : (4 + c) * own_high, :]
     for g in range(1, fields):
@@ -363,10 +377,10 @@
 
         return step
 
-    hess8 = lax.fori_loop(0, nodes, back(own_table, own_high, 0), jnp.zeros((8, elements), F32))
+    hess8 = each(nodes, back(own_table, own_high, 0), jnp.zeros((8, elements), F32))
     exchange_end(out_b, in_b, sems_b)
     ghosts_in(in_b)
-    hess8 = lax.fori_loop(0, nodes, back(ghost_table, ghost_high, owned), hess8)
+    hess8 = each(nodes, back(ghost_table, ghost_high, owned), hess8)
     hess = jnp.sum(hess8, axis=0, keepdims=True) + reg_weight[...] * search
 
     def lane_sums(values):

time: 31.9 us -> 29.5 us (0.925)
  Pallas kernels: 30.4 us -> 28 us
    pallas_call x1, Pallas kernels: 29 us -> 26.7 us  [on_device(): pl.pallas_call(functools.partial(kernel, doms, subs, fields, stages), out...]
where the time goes in v4:
time: 29.5 us; the launch traced here: 29.3 us
  Pallas kernels  28 us (95%)
  between operations  1.29 us (4%)
    pallas_call x1, Pallas kernels, on_device(): pl.pallas_call(functools.partial(kernel, doms, subs, fields, stages), out...  26.7 us
    pallas_call x1, Pallas kernels, on_device(): pl.pallas_call(hand_out, out_shape=[jax.ShapeDtypeStruct(row, F32)] * 3,...  1.33 us

profile of v4, /device:TPU:0, one launch (start us, length us, event | category | flops | bytes accessed | tf_op | source)
XLA Modules:
  0.0 29.3 jit_solution(5244482902450531758)
XLA Ops:
  1.3 26.7 %shard_map.139.result = f32[3,1,1024]{2,1,0:T(1,128)} custom-call(f32[3,4096]{1,0:T(4,128)} %background.1, f32[32,128]{1,0:T(8,128)} %bitcast.10, s32[10,1024]{1,0:T(8,128)} %connect.1, s32[1]{0:T(128)S(6)} %copy.15.live_blocks, f32[1,1024]{1,0:T(1,128)} %bitcast.11, f32[1,1024]{1,0:T(1,128)} %bitcast.12, f32[1,1024]{1,0:T(1,128)} %bitcast.13, ...), custom_call_target="tpu_custom_call" | custom-call | tf_op jit(solution)/shard_map/pallas_call | solution.py:501
  28.0 1.3 %shard_map.140 = (f32[1,1024]{1,0:T(1,128)}, f32[1,1024]{1,0:T(1,128)}, f32[1,1024]{1,0:T(1,128)}) custom-call(f32[3,1,1024]{2,1,0:T(1,128)} %shard_map.139.result), custom_call_target="tpu_custom_call" | custom-call | tf_op jit(solution)/shard_map/pallas_call | solution.py:537
